TPU v7x, 32 devices: a whole 2x2x4 slice. The times are simulated.
32 devices in a mesh: blk: 32 (over z, y, x, core).
Axes of the slice: x: 2, y: 2, z: 4, core: 2. Of those that a mesh axis runs over, the one named last changes fastest.
Arguments:
- node_latent: bfloat16 [131072, 128], P('blk'), may hold values from -16 to 16
- edge_latent: bfloat16 [786432, 128], P('blk'), may hold values from -6 to 6
- edge_ends: int32 [2, 786432], P(None, 'blk'), may hold values from 0 to 5631, as said below
- edge_owned: int32 [786432], P('blk'), may hold values from 0 to 1, as said below
- send_index: int32 [32, 6, 256], P('blk'), may hold values from 0 to 4095, as said below
- edge_w1: bfloat16 [2, 384, 128], replicated, may hold values from -0.3125 to 0.3125
- edge_b1: float32 [2, 128], replicated, may hold values from -3 to 3
- edge_w2: bfloat16 [2, 128, 128], replicated, may hold values from -0.5 to 0.5
- edge_gain: float32 [2, 128], replicated, may hold values from 0.5 to 1.5
- edge_shift: float32 [2, 128], replicated, may hold values from -2 to 2
- node_w1: bfloat16 [2, 256, 128], replicated, may hold values from -0.375 to 0.375
- node_b1: float32 [2, 128], replicated, may hold values from -3 to 3
- node_w2: bfloat16 [2, 128, 128], replicated, may hold values from -0.5 to 0.5
- node_gain: float32 [2, 128], replicated, may hold values from 0.5 to 1.5
- node_shift: float32 [2, 128], replicated, may hold values from -2 to 2
Outputs:
- node_out: bfloat16 [131072, 128], P('blk')
- edge_out: bfloat16 [786432, 128], P('blk')
Inputs may be any that keep to these rules, and one draw needn't show every extreme that they name: edge_ends[0] holds each slot's sender, edge_ends[1] its receiver, as entries of the block's extended node list. Slot s of a block lies in tile t = s // 128; each of its ends is either an own node from (t // 6) * 128 to (t // 6 + 1) * 128 - 1 or a halo entry from 4096 + (t % 6) * 256 to 4096 + (t % 6 + 1) * 256 - 1; at most one end of a slot is a halo entry. `edge_owned`: in each block the slots with 1 come first; every block has at least 15360 of them. send_index[b, k] lists 256 distinct nodes of block b.
All inputs are finite; a program needn't handle non-finite values.
Results may differ from a plain program's by a relative error of at most 0.0085.
Values may be sent and summed in bfloat16 or wider, within the bound.
A program may use at most 128 MiB of HBM per device.

v0:
```python
import functools

import jax
import jax.numpy as jnp
from jax import lax
from jax.experimental import pallas as pl
from jax.experimental.pallas import tpu as pltpu
from jax.sharding import PartitionSpec as P

LAYERS = 2
FACES = 6
GX = 4
GY = 4
MESH = pl.DeviceIdType.MESH
VMEM = pltpu.VMEM
F32 = jnp.float32
BF16 = jnp.bfloat16


def dot(a, b):
    return jnp.dot(a, b, preferred_element_type=F32)


def hot(mask):
    return jnp.where(mask, 1.0, 0.0).astype(BF16)


def iota(shape, axis):
    return lax.broadcasted_iota(jnp.int32, shape, axis)


def face_target(me, face, n, sign):
    step = jnp.where(face < 2, 1, jnp.where(face < 4, GX, GX * GY))
    step = jnp.where(face % 2 == 0, step, -step) * sign
    return lax.rem(me + step + n * GX * GY, n)


def edge_kernel(layer, own_rows, halo_rows, e_ref, ends_ref, owned_ref, tab_ref, phalo_ref,
                w1_ref, b1_ref, w2_ref, gain_ref, shift_ref,
                out_ref, own_ref, halo_ref, acc, bd1, bd2):
    step = pl.program_id(0)
    steps = pl.num_programs(0)
    tile = ends_ref.shape[3]
    width = e_ref.shape[1]
    rows = FACES * tile

    @pl.when(step == 0)
    def _():
        acc[...] = jnp.zeros_like(acc)
        bd1[...] = jnp.zeros_like(bd1)
        bd2[...] = jnp.zeros_like(bd2)
        for i in range(2):
            bd1[i * width:(i + 1) * width, i * width:(i + 1) * width] = w1_ref[layer, 0:width, :]
            bd2[i * width:(i + 1) * width, i * width:(i + 1) * width] = w2_ref[layer]

    per_step = ends_ref.shape[1]
    face = iota((FACES, tile), 0)
    lane = iota((rows, tile), 1)
    bias = b1_ref[layer:layer + 1, :]
    gain = gain_ref[layer:layer + 1, :]
    shift = shift_ref[layer:layer + 1, :]
    for pair in range(per_step // 2):
        hots, tables, recv_rows, halo_recv, flags_r, flags_o, pre = [], [], [], [], [], [], []
        halo_hots = []
        for i in range(2):
            local = pair * 2 + i
            group = step * per_step + local
            s = ends_ref[0, local]
            r = ends_ref[1, local]
            ok = owned_ref[local] > 0
            s_halo = s >= own_rows
            r_halo = r >= own_rows
            so = jnp.where(ok & ~s_halo, s - group * tile, 255)
            ro = jnp.where(ok & ~r_halo, r - group * tile, 255)
            base = own_rows + face * halo_rows
            hs = jnp.where(s_halo, s - base, jnp.where(r_halo, r - base, 511))
            hc = jnp.where(ok, hs, 511)
            recv_rows.append(ro)
            halo_recv.append(jnp.where(ok & r_halo, r - base, 511))
            code = (so | (ro << 8) | (hc << 16) | jnp.where(r_halo, 1 << 25, 0)
                    | jnp.where(ok, 1 << 26, 0))
            cols = jnp.concatenate(
                [jnp.broadcast_to(code[k:k + 1, :], (tile, tile)).T for k in range(FACES)], axis=0)
            sr = jnp.concatenate(
                [hot((cols & 255) == lane), hot(((cols >> 8) & 255) == lane)], axis=1)
            hcol = (cols >> 16) & 511
            halo_hots.append(jnp.concatenate([hot(hcol == lane + j * tile)
                                              for j in range(halo_rows // tile)], axis=1))
            flags_r.append((cols & (1 << 25)) != 0)
            flags_o.append((cols & (1 << 26)) != 0)
            pre.append(dot(sr, tab_ref[local]))
        from_halo = [[], []]
        for k in range(FACES):
            at = slice(k * tile, (k + 1) * tile)
            both = dot(jnp.concatenate([halo_hots[0][at], halo_hots[1][at]], axis=0), phalo_ref[k])
            for i in range(2):
                part = both[i * tile:(i + 1) * tile]
                from_halo[i].append(jnp.where(flags_r[i][at], part[:, width:], part[:, :width]))
        edges = [e_ref[(pair * 2 + i) * rows:(pair * 2 + i + 1) * rows, :] for i in range(2)]
        from_e = dot(jnp.concatenate(edges, axis=1), bd1[...])
        hidden = []
        for i in range(2):
            before = from_e[:, i * width:(i + 1) * width] + pre[i] + jnp.concatenate(from_halo[i], axis=0)
            hidden.append(jnp.maximum(before + bias, 0.0).astype(BF16))
        mixed2 = dot(jnp.concatenate(hidden, axis=1), bd2[...])
        fresh = []
        for i in range(2):
            mixed = mixed2[:, i * width:(i + 1) * width]
            centre = mixed - jnp.mean(mixed, axis=1, keepdims=True)
            spread = jnp.mean(centre * centre, axis=1, keepdims=True)
            normed = gain * (centre * lax.rsqrt(spread + 1e-05)) + shift
            new = (edges[i].astype(F32) + jnp.where(flags_o[i], normed, 0.0)).astype(BF16)
            out_ref[(pair * 2 + i) * rows:(pair * 2 + i + 1) * rows, :] = new
            fresh.append(new)
            node = iota((tile, tile), 0)
            hot_t = jnp.concatenate([hot(recv_rows[i][k:k + 1, :] == node) for k in range(FACES)], axis=1)
            own_ref[(pair * 2 + i) * tile:(pair * 2 + i + 1) * tile, :] = dot(hot_t, new)
        node = iota((halo_rows, tile), 0)
        for k in range(FACES):
            at = slice(k * tile, (k + 1) * tile)
            hot_t = jnp.concatenate([hot(halo_recv[i][k:k + 1, :] == node) for i in range(2)], axis=1)
            acc[k] += dot(hot_t, jnp.concatenate([fresh[0][at], fresh[1][at]], axis=0))

    @pl.when(step == steps - 1)
    def _():
        halo_ref[...] = acc[...].astype(BF16)


def edge_layer(layer, e, ends, owned, tab, phalo, w1, b1, w2, gain, shift, own_rows, halo_rows):
    groups, tile = ends.shape[1], ends.shape[3]
    width = e.shape[1]
    per = 4 if groups % 4 == 0 else 2
    rows = FACES * tile
    whole = lambda a: pl.BlockSpec(a.shape, lambda i: (0,) * a.ndim)
    return pl.pallas_call(
        functools.partial(edge_kernel, layer, own_rows, halo_rows),
        grid=(groups // per,),
        in_specs=[
            pl.BlockSpec((per * rows, width), lambda i: (i, 0)),
            pl.BlockSpec((2, per, FACES, tile), lambda i: (0, i, 0, 0)),
            pl.BlockSpec((per, FACES, tile), lambda i: (i, 0, 0)),
            pl.BlockSpec((per, 2 * tile, width), lambda i: (i, 0, 0)),
            whole(phalo), whole(w1), whole(b1), whole(w2), whole(gain), whole(shift),
        ],
        out_specs=[
            pl.BlockSpec((per * rows, width), lambda i: (i, 0)),
            pl.BlockSpec((per * tile, width), lambda i: (i, 0)),
            pl.BlockSpec((FACES, halo_rows, width), lambda i: (0, 0, 0)),
        ],
        out_shape=[
            jax.ShapeDtypeStruct(e.shape, BF16),
            jax.ShapeDtypeStruct((own_rows, width), F32),
            jax.ShapeDtypeStruct((FACES, halo_rows, width), BF16),
        ],
        scratch_shapes=[
            VMEM((FACES, halo_rows, width), F32),
            VMEM((2 * width, 2 * width), BF16),
            VMEM((2 * width, 2 * width), BF16),
        ],
        compiler_params=pltpu.CompilerParams(dimension_semantics=("arbitrary",)),
    )(e, ends, owned, tab, phalo, w1, b1, w2, gain, shift)


def first_weights(w1_ref, layer, width):
    return jnp.concatenate(
        [w1_ref[layer, width:2 * width, :], w1_ref[layer, 2 * width:3 * width, :]], axis=1)


def exchange_latents(me, n, layer, h_ref, send_ref, w1_ref, tab_ref, phalo_ref, stage, landed, ssem, rsem):
    own_rows, width = h_ref.shape
    halo_rows = send_ref.shape[1]
    tile = 128
    chunk = min(1024, own_rows)
    weights = first_weights(w1_ref, layer, width)

    def copy(k):
        return pltpu.make_async_remote_copy(
            src_ref=stage.at[k], dst_ref=landed.at[k], send_sem=ssem.at[k], recv_sem=rsem.at[k],
            device_id=(face_target(me, k, n, 1),), device_id_type=MESH)

    @pl.loop(0, FACES)
    def _(k):
        row = send_ref[pl.ds(k, 1), :]
        cols = jnp.concatenate(
            [jnp.broadcast_to(row[:, j * tile:(j + 1) * tile], (tile, tile)).T
             for j in range(halo_rows // tile)], axis=0)
        lane = iota(cols.shape, 1)
        total = None
        for c in range(own_rows // chunk):
            one = jnp.concatenate(
                [hot(cols == lane + (c * chunk + j * tile)) for j in range(chunk // tile)], axis=1)
            part = dot(one, h_ref[c * chunk:(c + 1) * chunk, :])
            total = part if total is None else total + part
        stage[pl.ds(k, 1)] = total.astype(BF16)[None]
        copy(k).start()

    @pl.loop(0, tab_ref.shape[0])
    def _(g):
        both = dot(h_ref[pl.ds(pl.multiple_of(g * tile, tile), tile), :], weights).astype(BF16)
        tab_ref[pl.ds(g, 1)] = jnp.concatenate([both[:, :width], both[:, width:]], axis=0)[None]

    @pl.loop(0, FACES)
    def _(k):
        copy(k).wait()
        phalo_ref[pl.ds(k, 1)] = dot(landed[k], weights).astype(BF16)[None]


def first_kernel(n, h_ref, send_ref, w1_ref, tab_ref, phalo_ref, stage, landed, ssem, rsem):
    me = lax.axis_index("blk")
    barrier = pltpu.get_barrier_semaphore()
    for k in range(FACES):
        pl.semaphore_signal(barrier, inc=1, device_id=(face_target(me, k, n, 1),), device_id_type=MESH)
    pl.semaphore_wait(barrier, FACES)
    exchange_latents(me, n, 0, h_ref, send_ref, w1_ref, tab_ref, phalo_ref, stage, landed, ssem, rsem)


def node_kernel(n, layer, last, h_ref, own_ref, halo_ref, send_ref, ew1_ref, w1_ref, b1_ref, w2_ref,
                gain_ref, shift_ref, *rest):
    if last:
        out_ref, returned, update, mine, stats, ssem, rsem, tsem, usem = rest
    else:
        (out_ref, tab_ref, phalo_ref, returned, update, mine, stats, ssem, rsem, tsem, usem,
         stage, landed, ssem2, rsem2) = rest
    me = lax.axis_index("blk")
    own_rows, width = h_ref.shape
    halo_rows = send_ref.shape[1]
    barrier = pltpu.get_barrier_semaphore()

    @pl.loop(1, n)
    def _(j):
        pl.semaphore_signal(barrier, inc=1, device_id=(lax.rem(me + j, n),), device_id_type=MESH)

    pl.semaphore_wait(barrier, n - 1)

    def copy(k):
        return pltpu.make_async_remote_copy(
            src_ref=halo_ref.at[k], dst_ref=returned.at[k], send_sem=ssem.at[k], recv_sem=rsem.at[k],
            device_id=(face_target(me, k, n, -1),), device_id_type=MESH)

    for k in range(FACES):
        copy(k).start()
    for k in range(FACES):
        copy(k).wait()
    back = returned[...].reshape(FACES * halo_rows, width)
    chunk = min(512, own_rows)

    def body(c, carry):
        sums, squares = carry
        first = pl.multiple_of(c * chunk, chunk)
        at = pl.ds(first, chunk)
        node = iota((chunk, halo_rows), 0) + first
        one = jnp.concatenate([hot(send_ref[k:k + 1, :] == node) for k in range(FACES)], axis=1)
        agg = (own_ref[at, :] + dot(one, back)).astype(BF16)
        joined = jnp.concatenate([h_ref[at, :], agg], axis=1)
        hidden = jnp.maximum(dot(joined, w1_ref[layer]) + b1_ref[layer:layer + 1, :], 0.0).astype(BF16)
        upd = dot(hidden, w2_ref[layer])
        update[at, :] = upd
        return (sums + jnp.sum(upd, axis=0, keepdims=True),
                squares + jnp.sum(upd * upd, axis=0, keepdims=True))

    zero = jnp.zeros((1, width), F32)
    sums, squares = lax.fori_loop(0, own_rows // chunk, body, (zero, zero))
    packed = jnp.concatenate([sums, squares, jnp.zeros((6, width), F32)], axis=0)
    mine[...] = packed
    stats[pl.ds(me, 1)] = packed[None]

    def share(j):
        return pltpu.make_async_remote_copy(
            src_ref=mine, dst_ref=stats.at[me], send_sem=tsem.at[j], recv_sem=usem.at[j],
            device_id=(lax.rem(me + j, n),), device_id_type=MESH)

    @pl.loop(1, n)
    def _(j):
        share(j).start()

    @pl.loop(1, n)
    def _(j):
        share(j).wait()

    total = jnp.sum(stats[...], axis=0)
    count = own_rows * n
    mean = total[0:1] / count
    variance = jnp.maximum(total[1:2] / count - mean * mean, 0.0)
    scale = gain_ref[layer:layer + 1, :] * lax.rsqrt(variance + 1e-05)
    shift = shift_ref[layer:layer + 1, :]

    @pl.loop(0, own_rows // chunk)
    def _(c):
        at = pl.ds(pl.multiple_of(c * chunk, chunk), chunk)
        out_ref[at, :] = (h_ref[at, :].astype(F32) + scale * (update[at, :] - mean) + shift).astype(BF16)

    if not last:
        exchange_latents(me, n, layer + 1, out_ref, send_ref, ew1_ref, tab_ref, phalo_ref,
                         stage, landed, ssem2, rsem2)


def per_device(n, node_latent, edge_latent, edge_ends, edge_owned, send_index, edge_w1, edge_b1, edge_w2,
               edge_gain, edge_shift, node_w1, node_b1, node_w2, node_gain, node_shift):
    own_rows, width = node_latent.shape
    halo_rows = send_index.shape[2]
    tile = 128
    groups = own_rows // tile
    ends = edge_ends.reshape(2, groups, FACES, tile)
    owned = edge_owned.reshape(groups, FACES, tile)
    send = send_index[0]
    tab_shape = jax.ShapeDtypeStruct((groups, 2 * tile, width), BF16)
    phalo_shape = jax.ShapeDtypeStruct((FACES, halo_rows, 2 * width), BF16)
    spec = pl.BlockSpec(memory_space=VMEM)
    faces = VMEM((FACES, halo_rows, width), BF16)
    sems = pltpu.SemaphoreType.DMA((FACES,))
    tab, phalo = pl.pallas_call(
        functools.partial(first_kernel, n),
        in_specs=[spec] * 3,
        out_specs=[spec] * 2,
        out_shape=[tab_shape, phalo_shape],
        scratch_shapes=[faces, faces, sems, sems],
        compiler_params=pltpu.CompilerParams(collective_id=0, has_side_effects=True),
    )(node_latent, send, edge_w1)
    latents, edges = node_latent, edge_latent
    for layer in range(LAYERS):
        edges, own_sums, halo_sums = edge_layer(
            layer, edges, ends, owned, tab, phalo, edge_w1, edge_b1, edge_w2, edge_gain, edge_shift,
            own_rows, halo_rows)
        last = layer == LAYERS - 1
        out = [jax.ShapeDtypeStruct((own_rows, width), BF16)]
        scratch = [faces, VMEM((own_rows, width), F32), VMEM((8, width), F32), VMEM((n, 8, width), F32),
                   sems, sems, pltpu.SemaphoreType.DMA((n,)), pltpu.SemaphoreType.DMA((n,))]
        if not last:
            out += [tab_shape, phalo_shape]
            scratch += [faces, faces, sems, sems]
        result = pl.pallas_call(
            functools.partial(node_kernel, n, layer, last),
            in_specs=[spec] * 10,
            out_specs=[spec] * len(out),
            out_shape=out,
            scratch_shapes=scratch,
            compiler_params=pltpu.CompilerParams(collective_id=1 + layer, has_side_effects=True),
        )(latents, own_sums, halo_sums, send, edge_w1, node_w1, node_b1, node_w2, node_gain, node_shift)
        latents = result[0]
        if not last:
            tab, phalo = result[1:]
    return (latents, edges)


def solution(mesh):
    row, rep = P("blk", None), P()
    return jax.shard_map(
        functools.partial(per_device, mesh.shape["blk"]),
        mesh=mesh,
        in_specs=(row, row, P(None, "blk"), P("blk"), P("blk", None, None)) + (rep,) * 10,
        out_specs=(row, row),
        check_vma=False,
    )
```

profile of v0, /device:TPU:0, one launch (start us, length us, event | category | flops | bytes accessed | tf_op | source)
XLA Modules:
  0.0 157.0 jit_solution(15975910743057662023)
XLA Ops:
  0.6 1.3 copy.19
  1.9 1.6 reshape.11.owned_ref
  3.5 1.8 %reshape.10.ends_ref = s32[2,32,6,128]{3,2,1,0:T(8,128)} reshape(s32[2,24576]{1,0:T(2,128)} %param.17) | data formatting | bytes 393216 | tf_op jit(solution)/shard_map/reshape | solution.py:303
  5.3 19.7 %shard_map.158 = (bf16[32,256,128]{2,1,0:T(8,128)(2,1)}, bf16[6,256,256]{2,1,0:T(8,128)(2,1)}) custom-call(bf16[4096,128]{1,0:T(8,128)(2,1)} %h_ref.3, s32[6,256]{1,0:T(8,128)} %bitcast.3, bf16[2,384,128]{2,1,0:T(8,128)(2,1)} %ew1_ref.3), custom_call_target="tpu_custom_call" | custom-call | tf_op jit(solution)/shard_map/pallas_call | solution.py:311
  25.0 28.8 %shard_map.159 = (bf16[24576,128]{1,0:T(8,128)(2,1)}, f32[4096,128]{1,0:T(8,128)}, bf16[6,256,128]{2,1,0:T(8,128)(2,1)}) custom-call(bf16[24576,128]{1,0:T(8,128)(2,1)} %e_ref.1, s32[2,32,6,128]{3,2,1,0:T(8,128)} %reshape.10.ends_ref, s32[32,6,128]{2,1,0:T(8,128)} %reshape.11.owned_ref, bf16[32,256,128]{2,1,0:T(8,128)(2,1)} %get-tuple-element.13.tab_ref, ...), custom_call_target="tpu_custom_call" | custom-call | tf_op jit(solution)/shard_map/pallas_call | solution.py:135
  53.7 43.4 %shard_map.160 = (bf16[4096,128]{1,0:T(8,128)(2,1)}, bf16[32,256,128]{2,1,0:T(8,128)(2,1)}, bf16[6,256,256]{2,1,0:T(8,128)(2,1)}) custom-call(bf16[4096,128]{1,0:T(8,128)(2,1)} %h_ref.3, f32[4096,128]{1,0:T(8,128)} %get-tuple-element.15.own_ref, bf16[6,256,128]{2,1,0:T(8,128)(2,1)} %get-tuple-element.16.halo_ref, s32[6,256]{1,0:T(8,128)} %bitcast.4, ...), custom_call_target="tpu_custom_call" | custom-call | tf_op jit(solution)/shard_map/pallas_call | solution.py:331
  97.2 28.8 %shard_map.161 = (bf16[24576,128]{1,0:T(8,128)(2,1)}, f32[4096,128]{1,0:T(8,128)}, bf16[6,256,128]{2,1,0:T(8,128)(2,1)}) custom-call(bf16[24576,128]{1,0:T(8,128)(2,1)} %get-tuple-element.18.e_ref, s32[2,32,6,128]{3,2,1,0:T(8,128)} %reshape.10.ends_ref, s32[32,6,128]{2,1,0:T(8,128)} %reshape.11.owned_ref, bf16[32,256,128]{2,1,0:T(8,128)(2,1)} %get-tuple-element.19.tab_ref, ...), custom_call_target="tpu_custom_call" | custom-call | tf_op jit(solution)/shard_map/pallas_call | solution.py:135
  125.9 28.8 %shard_map.162 = bf16[4096,128]{1,0:T(8,128)(2,1)} custom-call(bf16[4096,128]{1,0:T(8,128)(2,1)} %get-tuple-element.17.h_ref, f32[4096,128]{1,0:T(8,128)} %get-tuple-element.21.own_ref, bf16[6,256,128]{2,1,0:T(8,128)(2,1)} %get-tuple-element.22.halo_ref, s32[6,256]{1,0:T(8,128)} %bitcast.5, bf16[2,384,128]{2,1,0:T(8,128)(2,1)} %ew1_ref.3, ...), custom_call_target="tpu_custom_call" | custom-call | tf_op jit(solution)/shard_map/pallas_call | solution.py:331
  154.8 2.3 %copy.21 = bf16[4096,128]{1,0:T(8,128)(2,1)} copy(bf16[4096,128]{1,0:T(8,128)(2,1)} %shard_map.162) | data formatting | bytes 2097152
where the time goes:
time: 157 us
  Pallas kernels  149 us (95%)
  local copies, waits for them, and re-layouts  6.89 us (4%)
    pallas_call x2, Pallas kernels, per_device(): pl.pallas_call(functools.partial(node_kernel, n, layer, last), in_specs=[...  72.3 us
    pallas_call x2, Pallas kernels, edge_layer(): pl.pallas_call(functools.partial(edge_kernel, layer, own_rows, halo_rows)...  57.5 us
    pallas_call x1, Pallas kernels, per_device(): pl.pallas_call(functools.partial(first_kernel, n), in_specs=[spec] * 3, o...  19.7 us
    unnamed x2, local copies, waits for them, and re-layouts  3.55 us

commit v1 on v0

v1 whole, which is shorter than its diff:
```python
import functools

import jax
import jax.numpy as jnp
from jax import lax
from jax.experimental import pallas as pl
from jax.experimental.pallas import tpu as pltpu
from jax.sharding import PartitionSpec as P

LAYERS = 2
FACES = 6
GX = 4
GY = 4
TILE = 128
UNITS = 8
CHUNKS = 8
MESH = pl.DeviceIdType.MESH
VMEM = pltpu.VMEM
F32 = jnp.float32
BF16 = jnp.bfloat16
I32 = jnp.int32
I16 = jnp.int16


def dot(a, b):
    return jnp.dot(a, b, preferred_element_type=F32)


def dot_t(a, b):
    return lax.dot_general(a, b, (((1,), (1,)), ((), ())), preferred_element_type=F32)


def iota(shape, axis):
    return lax.broadcasted_iota(I32, shape, axis)


def hot_rows(row, rows):
    width = row.shape[1]
    wide = jnp.broadcast_to(row, (16, width)).astype(I16)
    wide = jnp.concatenate([wide] * (rows // 16), axis=0)
    return jnp.where(wide == iota((rows, width), 0).astype(I16), jnp.ones((), BF16), jnp.zeros((), BF16))


def column(row):
    return jnp.broadcast_to(row, (TILE, TILE)).T


def twice(block):
    return jnp.concatenate([block, block], axis=1)


def face_target(me, face, n, sign):
    step = jnp.where(face < 2, 1, jnp.where(face < 4, GX, GX * GY))
    step = jnp.where(face % 2 == 0, step, -step) * sign
    return lax.rem(me + step + n * GX * GY, n)


def mesh_kernel(n, h_ref, e_ref, ends_ref, owned_ref, send_ref, ew1_ref, eb1_ref, ew2_ref, egain_ref, eshift_ref,
                nw1_ref, nb1_ref, nw2_ref, ngain_ref, nshift_ref,
                hout_ref, eout_ref,
                ht, estage, et, hid, ptab, phalo, own_acc, halo_acc, upd, scol, w1e, w1sr, w2c, cols, nw1, nw2,
                stage, landed, hsend, returned, sums, mine, stats,
                esem, osem, lsend, lrecv, bsend, brecv, tsem, usem):
    me = lax.axis_index("blk")
    own_rows, width = h_ref.shape
    halo_rows = stage.shape[3]
    groups = own_rows // TILE
    barrier = pltpu.get_barrier_semaphore()

    @pl.loop(1, n)
    def _(j):
        pl.semaphore_signal(barrier, inc=1, device_id=(lax.rem(me + j, n),), device_id_type=MESH)

    edges_in = pltpu.make_async_copy(e_ref, estage, esem)
    edges_in.start()

    def latents_copy(layer, k):
        return pltpu.make_async_remote_copy(
            src_ref=stage.at[layer, k], dst_ref=landed.at[layer, k], send_sem=lsend.at[layer, k],
            recv_sem=lrecv.at[layer, k], device_id=(face_target(me, k, n, 1),), device_id_type=MESH)

    def sums_copy(layer, k):
        return pltpu.make_async_remote_copy(
            src_ref=hsend.at[layer, k], dst_ref=returned.at[layer, k], send_sem=bsend.at[layer, k],
            recv_sem=brecv.at[layer, k], device_id=(face_target(me, k, n, -1),), device_id_type=MESH)

    def stats_copy(layer, j):
        return pltpu.make_async_remote_copy(
            src_ref=mine.at[layer], dst_ref=stats.at[layer, me], send_sem=tsem.at[layer, j],
            recv_sem=usem.at[layer, j], device_id=(lax.rem(me + j, n),), device_id_type=MESH)

    def edges_out(q):
        at = pl.ds(2 * q, 2)
        return pltpu.make_async_copy(et.at[:, at], eout_ref.at[:, at], osem.at[q])

    for j in range(groups // 4):
        for i in range(j * 4, j * 4 + 4):
            ht[:, i * TILE:(i + 1) * TILE] = h_ref[i * TILE:(i + 1) * TILE, :].T
    for j in range(FACES * halo_rows // TILE):
        row = send_ref[0:1, j * TILE:(j + 1) * TILE]
        scol[j * TILE:(j + 1) * TILE, :] = column(row).astype(I16)

    def gather(layer, k0):
        totals = [None] * 2
        rows = [send_ref[0:1, pl.ds(pl.multiple_of((k0 + f) * halo_rows, TILE), halo_rows)] for f in range(2)]
        for b in range(own_rows // 256):
            for f in range(2):
                part = dot(ht[:, b * 256:(b + 1) * 256], hot_rows(rows[f] - b * 256, 256))
                totals[f] = part if totals[f] is None else totals[f] + part
        for f in range(2):
            stage[layer, pl.ds(k0 + f, 1)] = totals[f].astype(BF16)[None]
            latents_copy(layer, k0 + f).start()

    def load_edge_weights(layer):
        w1e[...] = ew1_ref[layer, 0:width, :].T
        w1sr[0:width, :] = ew1_ref[layer, width:2 * width, :].T
        w1sr[width:2 * width, :] = ew1_ref[layer, 2 * width:3 * width, :].T
        second = ew2_ref[layer].astype(F32).T
        second = second - jnp.mean(second, axis=0, keepdims=True)
        w2c[...] = second.astype(BF16)
        cols[0] = column(0.5 * eb1_ref[layer:layer + 1, :])
        cols[1] = column(egain_ref[layer:layer + 1, :])
        cols[2] = column(eshift_ref[layer:layer + 1, :])

    def load_node_weights(layer):
        nw1[...] = nw1_ref[layer].T
        nw2[...] = nw2_ref[layer].T
        cols[3] = column(nb1_ref[layer:layer + 1, :])

    def own_tables():
        chunk = 4 * TILE

        @pl.loop(0, own_rows // chunk // 2)
        def _(c):
            for half in range(2):
                first = pl.multiple_of((c * 2 + half) * chunk, chunk)
                both = dot(w1sr[...], ht[:, pl.ds(first, chunk)])
                both = (both + twice(twice(jnp.concatenate([cols[0], cols[0]], axis=0)))).astype(BF16)
                for j in range(4):
                    at = slice(j * TILE, (j + 1) * TILE)
                    ptab[pl.ds((c * 2 + half) * 4 + j, 1)] = jnp.concatenate(
                        [both[:width, at], both[width:, at]], axis=1)[None]
                    own_acc[pl.ds((c * 2 + half) * 4 + j, 1)] = jnp.zeros((1, TILE, TILE), F32)

    def ends_of(group, face):
        first = pl.multiple_of((group * FACES + face) * TILE, TILE)
        s = ends_ref[0:1, pl.ds(first, TILE)]
        r = ends_ref[1:2, pl.ds(first, TILE)]
        ok = owned_ref[0:1, pl.ds(first, TILE)] > 0
        return s, r, ok, r >= own_rows

    def both_tiles(pick, group, k0):
        return jnp.concatenate([pick(group, k0), pick(group, k0 + 1)], axis=1)

    def send_row(group, face):
        s, _, _, _ = ends_of(group, face)
        return jnp.where(s >= own_rows, -1, s - group * TILE)

    def receive_row(group, face):
        _, r, ok, r_halo = ends_of(group, face)
        return jnp.where(ok & ~r_halo, r - group * TILE, -1)

    def halo_row(group, face):
        s, r, ok, r_halo = ends_of(group, face)
        return jnp.where(ok, jnp.where(r_halo, r, s) - (own_rows + face * halo_rows), -1)

    def halo_flag(group, face):
        _, _, ok, r_halo = ends_of(group, face)
        return jnp.where(ok & r_halo, 1.0, 0.0)

    def halo_receive_row(group, face):
        _, r, ok, r_halo = ends_of(group, face)
        return jnp.where(ok & r_halo, r - (own_rows + face * halo_rows), -1)

    def both_groups(pick, pair, face):
        return jnp.concatenate([pick(pair * 2, face), pick(pair * 2 + 1, face)], axis=1)

    def gather_stage(layer, u, pair, k0):
        from_halo = [[None] * 2, [None] * 2]
        for f in range(2):
            both = dot(phalo[f], hot_rows(both_groups(halo_row, pair, k0 + f), halo_rows))
            for g in range(2):
                part = both[:, g * TILE:(g + 1) * TILE]
                flag = jnp.broadcast_to(halo_flag(pair * 2 + g, k0 + f), (width, TILE)) > 0.5
                from_halo[g][f] = jnp.where(flag, part[width:], part[:width])
        for g in range(2):
            group = pair * 2 + g
            old = []
            for f in range(2):
                if layer == 0:
                    first = pl.multiple_of((group * FACES + k0 + f) * TILE, TILE)
                    old.append(estage[pl.ds(first, TILE), :].T)
                    et[group, k0 + f] = old[f]
                else:
                    old.append(et[group, k0 + f])
            hots = jnp.concatenate([hot_rows(both_tiles(send_row, group, k0), TILE),
                                    hot_rows(both_tiles(receive_row, group, k0), TILE),
                                    jnp.concatenate(old, axis=1)], axis=0)
            before = dot(jnp.concatenate([ptab[group], w1e[...]], axis=1), hots)
            before = before + jnp.concatenate(from_halo[g], axis=1)
            hid[u, g] = jnp.maximum(before, 0.0).astype(BF16)

    def mix_stage(layer, u, pair, k0):
        for g in range(2):
            group = pair * 2 + g
            centre = dot(w2c[...], hid[u, g])
            spread = jnp.mean(centre * centre, axis=0, keepdims=True)
            ok = jnp.concatenate([owned_ref[0:1, pl.ds(pl.multiple_of((group * FACES + k0 + f) * TILE, TILE), TILE)]
                                  for f in range(2)], axis=1)
            keep = jnp.broadcast_to(ok, centre.shape) > 0
            normed = twice(cols[1]) * (centre * lax.rsqrt(spread + 1e-05)) + twice(cols[2])
            old = jnp.concatenate([et[group, k0], et[group, k0 + 1]], axis=1)
            new = (old.astype(F32) + jnp.where(keep, normed, 0.0)).astype(BF16)
            for f in range(2):
                et[group, k0 + f] = new[:, f * TILE:(f + 1) * TILE]

    def scatter_stage(pairs, k0):
        for pair in pairs:
            for g in range(2):
                group = pair * 2 + g
                new = jnp.concatenate([et[group, k0], et[group, k0 + 1]], axis=1)
                own_acc[group] += dot_t(new, hot_rows(both_tiles(receive_row, group, k0), TILE))
        for f in range(2):
            sent = jnp.concatenate([et[pair * 2 + g, k0 + f] for pair in pairs for g in range(2)], axis=1)
            hots = jnp.concatenate([hot_rows(both_groups(halo_receive_row, pair, k0 + f), halo_rows) for pair in pairs], axis=1)
            halo_acc[f] += dot_t(sent, hots)

    def edge_phase(layer, q):
        k0 = 2 * q
        for f in range(2):
            latents_copy(layer, k0 + f).wait_recv()
            half_bias = twice(jnp.concatenate([cols[0], cols[0]], axis=0))
            phalo[f] = (dot(w1sr[...], landed[layer, k0 + f]) + half_bias).astype(BF16)
        halo_acc[...] = jnp.zeros_like(halo_acc)
        steps = groups // 2 // UNITS

        def units(i):
            return [i * UNITS + u for u in range(UNITS)]

        def stage_one(i):
            for u, pair in enumerate(units(i)):
                gather_stage(layer, u, pair, k0)

        def stage_two(i):
            for u, pair in enumerate(units(i)):
                mix_stage(layer, u, pair, k0)

        def stage_three(i):
            scatter_stage(units(i), k0)

        @pl.loop(0, steps)
        def _(i):
            stage_one(i)
            stage_two(i)
            stage_three(i)

        for f in range(2):
            hsend[layer, pl.ds(k0 + f, 1)] = halo_acc[f].astype(BF16)[None]
            sums_copy(layer, k0 + f).start()
        if layer == LAYERS - 1:
            edges_out(q).start()

    def slots(layer, faces, base):
        lane = iota((halo_rows, TILE), 1)
        hots = []
        for j in range(2):
            goal = (lane + (base + j * TILE)).astype(I16)
            hots.append(jnp.concatenate(
                [jnp.where(scol[k * halo_rows:(k + 1) * halo_rows, :] == goal, jnp.ones((), BF16), jnp.zeros((), BF16))
                 for k in faces], axis=0))
        values = jnp.concatenate([returned[layer, k] for k in faces], axis=1)
        return dot(values, jnp.concatenate(hots, axis=1))

    def early_sums(layer, faces):
        for k in faces:
            sums_copy(layer, k).wait_recv()

        @pl.loop(0, own_rows // 256 // CHUNKS)
        def _(c):
            for i in range(CHUNKS):
                pair = c * CHUNKS + i
                extra = slots(layer, faces, pair * 256)
                own_acc[pair * 2] += extra[:, :TILE]
                own_acc[pair * 2 + 1] += extra[:, TILE:]

    def node_mlp(layer, faces):
        for k in faces:
            sums_copy(layer, k).wait_recv()
        sums[...] = jnp.zeros_like(sums)

        @pl.loop(0, own_rows // 256 // CHUNKS)
        def _(c):
            joined, hidden = [], []
            for i in range(CHUNKS):
                pair = c * CHUNKS + i
                own = jnp.concatenate([own_acc[pair * 2], own_acc[pair * 2 + 1]], axis=1)
                agg = (own + slots(layer, faces, pair * 256)).astype(BF16)
                at = pl.ds(pl.multiple_of(pair * 256, 256), 256)
                joined.append(jnp.concatenate([ht[:, at], agg], axis=0))
            for i in range(CHUNKS):
                hidden.append(jnp.maximum(dot(nw1[...], joined[i]) + twice(cols[3]), 0.0).astype(BF16))
            for i in range(CHUNKS):
                update = dot(nw2[...], hidden[i])
                upd[:, pl.ds(pl.multiple_of((c * CHUNKS + i) * 256, 256), 256)] = update
                square = update * update
                sums[0] += update[:, :TILE] + update[:, TILE:]
                sums[1] += square[:, :TILE] + square[:, TILE:]

        packed = jnp.concatenate([jnp.sum(sums[i].T, axis=0, keepdims=True) for i in range(2)], axis=0)
        mine[layer] = packed
        stats[layer, pl.ds(me, 1)] = packed[None]

        @pl.loop(1, n)
        def _(j):
            stats_copy(layer, j).start()

    def node_norm(layer, target):
        @pl.loop(1, n)
        def _(j):
            stats_copy(layer, j).wait()

        total = jnp.sum(stats[layer], axis=0)
        count = own_rows * n
        mean = total[0:1] / count
        variance = jnp.maximum(total[1:2] / count - mean * mean, 0.0)
        scale = ngain_ref[layer:layer + 1, :] * lax.rsqrt(variance + 1e-05)
        cols[4] = column(scale)
        cols[5] = column(nshift_ref[layer:layer + 1, :] - scale * mean)

        @pl.loop(0, own_rows // 512)
        def _(c):
            for half in range(2):
                at = pl.ds(pl.multiple_of((c * 2 + half) * 256, 256), 256)
                target[:, at] = (ht[:, at].astype(F32) + twice(cols[4]) * upd[:, at] + twice(cols[5])).astype(BF16)

    load_edge_weights(0)
    load_node_weights(0)
    pl.semaphore_wait(barrier, n - 1)
    for layer in range(LAYERS):
        @pl.loop(0, FACES // 2)
        def _(p):
            gather(layer, 2 * lax.rem(p + 1, FACES // 2))

        own_tables()
        if layer == 0:
            edges_in.wait()

        @pl.loop(0, FACES // 2)
        def _(p):
            edge_phase(layer, lax.rem(p + 1, FACES // 2))

        early_sums(layer, (2, 3, 4, 5))
        node_mlp(layer, (0, 1))
        if layer < LAYERS - 1:
            load_edge_weights(layer + 1)
            load_node_weights(layer + 1)
        node_norm(layer, hout_ref if layer == LAYERS - 1 else ht)

        @pl.loop(0, FACES)
        def _(k):
            latents_copy(layer, k).wait_send()
            sums_copy(layer, k).wait_send()

    @pl.loop(0, FACES // 2)
    def _(q):
        edges_out(q).wait()


def turn_kernel(ht_ref, et_ref, h_ref, e_ref):
    width = ht_ref.shape[0]
    for i in range(ht_ref.shape[1] // TILE):
        h_ref[i * TILE:(i + 1) * TILE, :] = ht_ref[:, i * TILE:(i + 1) * TILE].T
        for k in range(FACES):
            first = (i * FACES + k) * TILE
            e_ref[first:first + TILE, :] = et_ref[i, k].T


def per_device(n, node_latent, edge_latent, edge_ends, edge_owned, send_index, edge_w1, edge_b1, edge_w2,
               edge_gain, edge_shift, node_w1, node_b1, node_w2, node_gain, node_shift):
    own_rows, width = node_latent.shape
    slots = edge_latent.shape[0]
    halo_rows = send_index.shape[2]
    groups = own_rows // TILE
    vmem = pl.BlockSpec(memory_space=VMEM)
    anywhere = pl.BlockSpec(memory_space=pl.ANY)
    faces = (LAYERS, FACES, width, halo_rows)
    sems = pltpu.SemaphoreType.DMA((LAYERS, FACES))
    peers = pltpu.SemaphoreType.DMA((LAYERS, n))
    ht, et = pl.pallas_call(
        functools.partial(mesh_kernel, n),
        in_specs=[vmem, anywhere] + [vmem] * 13,
        out_specs=[vmem, anywhere],
        out_shape=[jax.ShapeDtypeStruct((width, own_rows), BF16),
                   jax.ShapeDtypeStruct((groups, FACES, width, TILE), BF16)],
        scratch_shapes=[
            VMEM((width, own_rows), BF16),
            VMEM((slots, width), BF16),
            VMEM((groups, FACES, width, TILE), BF16),
            VMEM((UNITS, 2, width, 2 * TILE), BF16),
            VMEM((groups, width, 2 * TILE), BF16),
            VMEM((2, 2 * width, halo_rows), BF16),
            VMEM((groups, width, TILE), F32),
            VMEM((2, width, halo_rows), F32),
            VMEM((width, own_rows), F32),
            VMEM((FACES * halo_rows, TILE), I16),
            VMEM((width, width), BF16),
            VMEM((2 * width, width), BF16),
            VMEM((width, width), BF16),
            VMEM((6, width, TILE), F32),
            VMEM((width, 2 * width), BF16),
            VMEM((width, width), BF16),
            VMEM(faces, BF16), VMEM(faces, BF16), VMEM(faces, BF16), VMEM(faces, BF16),
            VMEM((2, width, TILE), F32), VMEM((LAYERS, 2, width), F32), VMEM((LAYERS, n, 2, width), F32),
            pltpu.SemaphoreType.DMA, pltpu.SemaphoreType.DMA((FACES // 2,)),
            sems, sems, sems, sems, peers, peers,
        ],
        compiler_params=pltpu.CompilerParams(collective_id=0, has_side_effects=True),
    )(node_latent, edge_latent, edge_ends, edge_owned.reshape(1, slots), send_index.reshape(1, FACES * halo_rows),
      edge_w1, edge_b1, edge_w2, edge_gain, edge_shift, node_w1, node_b1, node_w2, node_gain, node_shift)
    per = 4 if groups % 4 == 0 else 1
    return pl.pallas_call(
        turn_kernel,
        grid=(groups // per,),
        in_specs=[pl.BlockSpec((width, per * TILE), lambda i: (0, i)),
                  pl.BlockSpec((per, FACES, width, TILE), lambda i: (i, 0, 0, 0))],
        out_specs=[pl.BlockSpec((per * TILE, width), lambda i: (i, 0)),
                   pl.BlockSpec((per * FACES * TILE, width), lambda i: (i, 0))],
        out_shape=[jax.ShapeDtypeStruct((own_rows, width), BF16),
                   jax.ShapeDtypeStruct((slots, width), BF16)],
        compiler_params=pltpu.CompilerParams(dimension_semantics=("arbitrary",)),
    )(ht, et)


def solution(mesh):
    row, rep = P("blk", None), P()
    return jax.shard_map(
        functools.partial(per_device, mesh.shape["blk"]),
        mesh=mesh,
        in_specs=(row, row, P(None, "blk"), P("blk"), P("blk", None, None)) + (rep,) * 10,
        out_specs=(row, row),
        check_vma=False,
    )
```

time: 157 us -> 95 us (0.61)
  Pallas kernels: 149 us -> 94 us
  local copies, waits for them, and re-layouts: 6.89 us -> 0 us
    pallas_call x5 -> x2, Pallas kernels: 149 us -> 94 us  [the longest x1 85 us: per_device(): pl.pallas_call(functools.partial(mesh_kernel, n), in_specs=[vmem, anywher...]
    unnamed x2 -> x0, local copies, waits for them, and re-layouts: 3.55 us -> none
    reshape x2 -> x0, local copies, waits for them, and re-layouts: 3.34 us -> none  [the longest x1 1.79 us: per_device(): ends = edge_ends.reshape(2, groups, FACES, tile)]
where the time goes in v1:
time: 95 us; the launch traced here: 94.7 us
  Pallas kernels  94 us (99%)
    pallas_call x1, Pallas kernels, per_device(): pl.pallas_call(functools.partial(mesh_kernel, n), in_specs=[vmem, anywher...  85 us
    pallas_call x1, Pallas kernels, per_device(): pl.pallas_call(turn_kernel, grid=(groups // per,), in_specs=[pl.BlockSpec...  9.04 us

profile of v1, /device:TPU:0, one launch (start us, length us, event | category | flops | bytes accessed | tf_op | source)
XLA Modules:
  0.0 94.7 jit_solution(15596936326458606867)
XLA Ops:
  0.6 85.0 %shard_map.158 = (bf16[128,4096]{1,0:T(8,128)(2,1)}, bf16[32,6,128,128]{3,2,1,0:T(8,128)(2,1)}) custom-call(bf16[4096,128]{1,0:T(8,128)(2,1)} %h_ref.1, bf16[24576,128]{1,0:T(8,128)(2,1)} %e_ref.1, s32[2,24576]{1,0:T(2,128)} %ends_ref.1, s32[1,24576]{1,0:T(1,128)} %bitcast.2, s32[1,1536]{1,0:T(1,128)} %bitcast.3, bf16[2,384,128]{2,1,0:T(8,128)(2,1)} %ew1_ref.1, ...), custom_call_target="tpu_custom_call" | custom-call | tf_op jit(solution)/shard_map/pallas_call | solution.py:389
  85.6 9.0 %shard_map.159 = (bf16[4096,128]{1,0:T(8,128)(2,1)}, bf16[24576,128]{1,0:T(8,128)(2,1)}) custom-call(bf16[128,4096]{1,0:T(8,128)(2,1)} %get-tuple-element.4.ht_ref, bf16[32,6,128,128]{3,2,1,0:T(8,128)(2,1)} %get-tuple-element.5.et_ref), custom_call_target="tpu_custom_call" | custom-call | tf_op jit(solution)/shard_map/pallas_call | solution.py:421

commit v2 on v1

--- a/solution.py
+++ b/solution.py
@@ -12,7 +12,9 @@
 GX = 4
 GY = 4
 TILE = 128
-UNITS = 8
+UNITS = 16
+LAG = 2
+SPAN = 2
 CHUNKS = 8
 MESH = pl.DeviceIdType.MESH
 VMEM = pltpu.VMEM
@@ -49,18 +51,32 @@
     return jnp.concatenate([block, block], axis=1)
 
 
+def face_pair(phase):
+    return lax.rem(2 * phase, FACES // 2)
+
+
 def face_target(me, face, n, sign):
     step = jnp.where(face < 2, 1, jnp.where(face < 4, GX, GX * GY))
     step = jnp.where(face % 2 == 0, step, -step) * sign
     return lax.rem(me + step + n * GX * GY, n)
 
 
-def mesh_kernel(n, h_ref, e_ref, ends_ref, owned_ref, send_ref, ew1_ref, eb1_ref, ew2_ref, egain_ref, eshift_ref,
+def mesh_kernel(n, h_in, e_ref, ends_in, owned_in, send_in, ew1_in, eb1_in, ew2_in, egain_in, eshift_in,
+                nw1_in, nb1_in, nw2_in, ngain_in, nshift_in,
+                hout_ref, et,
+                h_ref, ends_ref, owned_ref, send_ref, ew1_ref, eb1_ref, ew2_ref, egain_ref, eshift_ref,
                 nw1_ref, nb1_ref, nw2_ref, ngain_ref, nshift_ref,
-                hout_ref, eout_ref,
-                ht, estage, et, hid, ptab, phalo, own_acc, halo_acc, upd, scol, w1e, w1sr, w2c, cols, nw1, nw2,
+                ht, ahead, estage, hid, ptab, phalo, own_acc, halo_acc, upd, scol, w1e, w1sr, w2c, cols, nw1, nw2,
                 stage, landed, hsend, returned, sums, mine, stats,
-                esem, osem, lsend, lrecv, bsend, brecv, tsem, usem):
+                esem, isem, lsend, lrecv, bsend, brecv, tsem, usem):
+    inputs = [(h_in, h_ref), (send_in, send_ref), (ew1_in, ew1_ref), (eb1_in, eb1_ref), (ew2_in, ew2_ref),
+              (egain_in, egain_ref), (eshift_in, eshift_ref), (nw1_in, nw1_ref), (nb1_in, nb1_ref), (nw2_in, nw2_ref),
+              (ngain_in, ngain_ref), (nshift_in, nshift_ref), (ends_in, ends_ref), (owned_in, owned_ref)]
+    loads = [pltpu.make_async_copy(source, target, isem.at[i]) for i, (source, target) in enumerate(inputs)]
+    for load in loads:
+        load.start()
+    edges_in = pltpu.make_async_copy(e_ref, estage, esem)
+    edges_in.start()
     me = lax.axis_index("blk")
     own_rows, width = h_ref.shape
     halo_rows = stage.shape[3]
@@ -71,9 +87,6 @@
     def _(j):
         pl.semaphore_signal(barrier, inc=1, device_id=(lax.rem(me + j, n),), device_id_type=MESH)
 
-    edges_in = pltpu.make_async_copy(e_ref, estage, esem)
-    edges_in.start()
-
     def latents_copy(layer, k):
         return pltpu.make_async_remote_copy(
             src_ref=stage.at[layer, k], dst_ref=landed.at[layer, k], send_sem=lsend.at[layer, k],
@@ -89,27 +102,57 @@
             src_ref=mine.at[layer], dst_ref=stats.at[layer, me], send_sem=tsem.at[layer, j],
             recv_sem=usem.at[layer, j], device_id=(lax.rem(me + j, n),), device_id_type=MESH)
 
-    def edges_out(q):
-        at = pl.ds(2 * q, 2)
-        return pltpu.make_async_copy(et.at[:, at], eout_ref.at[:, at], osem.at[q])
-
-    for j in range(groups // 4):
-        for i in range(j * 4, j * 4 + 4):
-            ht[:, i * TILE:(i + 1) * TILE] = h_ref[i * TILE:(i + 1) * TILE, :].T
+    loads[0].wait()
+    for i in range(groups):
+        ht[0:width, i * TILE:(i + 1) * TILE] = h_ref[i * TILE:(i + 1) * TILE, :].T
+    for load in loads[1:]:
+        load.wait()
     for j in range(FACES * halo_rows // TILE):
         row = send_ref[0:1, j * TILE:(j + 1) * TILE]
         scol[j * TILE:(j + 1) * TILE, :] = column(row).astype(I16)
 
-    def gather(layer, k0):
+    def gather(k0, rows):
         totals = [None] * 2
-        rows = [send_ref[0:1, pl.ds(pl.multiple_of((k0 + f) * halo_rows, TILE), halo_rows)] for f in range(2)]
+        picks = [send_ref[0:1, pl.ds(pl.multiple_of((k0 + f) * halo_rows, TILE), halo_rows)] for f in range(2)]
         for b in range(own_rows // 256):
             for f in range(2):
-                part = dot(ht[:, b * 256:(b + 1) * 256], hot_rows(rows[f] - b * 256, 256))
+                part = dot(ht[0:rows, b * 256:(b + 1) * 256], hot_rows(picks[f] - b * 256, 256))
                 totals[f] = part if totals[f] is None else totals[f] + part
-        for f in range(2):
-            stage[layer, pl.ds(k0 + f, 1)] = totals[f].astype(BF16)[None]
-            latents_copy(layer, k0 + f).start()
+        return totals
+
+    def send_first():
+        for phase in range(FACES // 2):
+            k0 = 2 * (2 * phase % (FACES // 2))
+            totals = gather(k0, width)
+            if phase == 0:
+                pl.semaphore_wait(barrier, n - 1)
+            for f in range(2):
+                stage[0, k0 + f] = totals[f].astype(BF16)
+                latents_copy(0, k0 + f).start()
+
+    def gather_ahead():
+        @pl.loop(0, FACES // 2)
+        def _(q):
+            totals = gather(2 * q, 2 * width)
+            for f in range(2):
+                ahead[2 * q + f] = totals[f]
+
+    def send_next(layer):
+        @pl.loop(0, FACES // 2)
+        def _(p):
+            k0 = 2 * face_pair(p)
+            for f in range(2):
+                new = ahead[k0 + f, 0:width] + twice(cols[4]) * ahead[k0 + f, width:2 * width] + twice(cols[5])
+                stage[layer, pl.ds(k0 + f, 1)] = new.astype(BF16)[None]
+                latents_copy(layer, k0 + f).start()
+
+    def turn_edges():
+        @pl.loop(0, groups // 2)
+        def _(i):
+            turned = [et[i * 2 + g, k].T for g in range(2) for k in range(FACES)]
+            for g in range(2):
+                for k in range(FACES):
+                    et[i * 2 + g, k] = turned[g * FACES + k]
 
     def load_edge_weights(layer):
         w1e[...] = ew1_ref[layer, 0:width, :].T
@@ -134,7 +177,7 @@
         def _(c):
             for half in range(2):
                 first = pl.multiple_of((c * 2 + half) * chunk, chunk)
-                both = dot(w1sr[...], ht[:, pl.ds(first, chunk)])
+                both = dot(w1sr[...], ht[0:width, pl.ds(first, chunk)])
                 both = (both + twice(twice(jnp.concatenate([cols[0], cols[0]], axis=0)))).astype(BF16)
                 for j in range(4):
                     at = slice(j * TILE, (j + 1) * TILE)
@@ -232,33 +275,21 @@
             half_bias = twice(jnp.concatenate([cols[0], cols[0]], axis=0))
             phalo[f] = (dot(w1sr[...], landed[layer, k0 + f]) + half_bias).astype(BF16)
         halo_acc[...] = jnp.zeros_like(halo_acc)
-        steps = groups // 2 // UNITS
-
-        def units(i):
-            return [i * UNITS + u for u in range(UNITS)]
-
-        def stage_one(i):
-            for u, pair in enumerate(units(i)):
-                gather_stage(layer, u, pair, k0)
-
-        def stage_two(i):
-            for u, pair in enumerate(units(i)):
-                mix_stage(layer, u, pair, k0)
-
-        def stage_three(i):
-            scatter_stage(units(i), k0)
-
-        @pl.loop(0, steps)
+
+        @pl.loop(0, groups // 2 // UNITS)
         def _(i):
-            stage_one(i)
-            stage_two(i)
-            stage_three(i)
+            for slot in range(UNITS + 2 * LAG + SPAN - 1):
+                if slot < UNITS:
+                    gather_stage(layer, slot, i * UNITS + slot, k0)
+                if 0 <= slot - LAG < UNITS:
+                    mix_stage(layer, slot - LAG, i * UNITS + slot - LAG, k0)
+                done = slot - 2 * LAG + 1
+                if 0 < done <= UNITS and done % SPAN == 0:
+                    scatter_stage([i * UNITS + u for u in range(done - SPAN, done)], k0)
 
         for f in range(2):
             hsend[layer, pl.ds(k0 + f, 1)] = halo_acc[f].astype(BF16)[None]
             sums_copy(layer, k0 + f).start()
-        if layer == LAYERS - 1:
-            edges_out(q).start()
 
     def slots(layer, faces, base):
         lane = iota((halo_rows, TILE), 1)
@@ -296,12 +327,15 @@
                 own = jnp.concatenate([own_acc[pair * 2], own_acc[pair * 2 + 1]], axis=1)
                 agg = (own + slots(layer, faces, pair * 256)).astype(BF16)
                 at = pl.ds(pl.multiple_of(pair * 256, 256), 256)
-                joined.append(jnp.concatenate([ht[:, at], agg], axis=0))
+                joined.append(jnp.concatenate([ht[0:width, at], agg], axis=0))
             for i in range(CHUNKS):
                 hidden.append(jnp.maximum(dot(nw1[...], joined[i]) + twice(cols[3]), 0.0).astype(BF16))
             for i in range(CHUNKS):
                 update = dot(nw2[...], hidden[i])
-                upd[:, pl.ds(pl.multiple_of((c * CHUNKS + i) * 256, 256), 256)] = update
+                at = pl.ds(pl.multiple_of((c * CHUNKS + i) * 256, 256), 256)
+                upd[:, at] = update
+                if layer < LAYERS - 1:
+                    ht[width:2 * width, at] = update.astype(BF16)
                 square = update * update
                 sums[0] += update[:, :TILE] + update[:, TILE:]
                 sums[1] += square[:, :TILE] + square[:, TILE:]
@@ -314,7 +348,13 @@
         def _(j):
             stats_copy(layer, j).start()
 
-    def node_norm(layer, target):
+    def node_norm(layer):
+        last = layer == LAYERS - 1
+        if last:
+            turn_edges()
+        else:
+            gather_ahead()
+
         @pl.loop(1, n)
         def _(j):
             stats_copy(layer, j).wait()
@@ -326,53 +366,55 @@
         scale = ngain_ref[layer:layer + 1, :] * lax.rsqrt(variance + 1e-05)
         cols[4] = column(scale)
         cols[5] = column(nshift_ref[layer:layer + 1, :] - scale * mean)
+        if not last:
+            send_next(layer + 1)
 
         @pl.loop(0, own_rows // 512)
         def _(c):
             for half in range(2):
                 at = pl.ds(pl.multiple_of((c * 2 + half) * 256, 256), 256)
-                target[:, at] = (ht[:, at].astype(F32) + twice(cols[4]) * upd[:, at] + twice(cols[5])).astype(BF16)
+                new = (ht[0:width, at].astype(F32) + twice(cols[4]) * upd[:, at] + twice(cols[5])).astype(BF16)
+                if last:
+                    hout_ref[at, :] = new.T
+                else:
+                    ht[0:width, at] = new
 
     load_edge_weights(0)
     load_node_weights(0)
-    pl.semaphore_wait(barrier, n - 1)
+    send_first()
     for layer in range(LAYERS):
-        @pl.loop(0, FACES // 2)
-        def _(p):
-            gather(layer, 2 * lax.rem(p + 1, FACES // 2))
-
         own_tables()
         if layer == 0:
             edges_in.wait()
 
         @pl.loop(0, FACES // 2)
         def _(p):
-            edge_phase(layer, lax.rem(p + 1, FACES // 2))
-
-        early_sums(layer, (2, 3, 4, 5))
-        node_mlp(layer, (0, 1))
+            edge_phase(layer, face_pair(p))
+
+        early_sums(layer, (0, 1))
+        early_sums(layer, (4, 5))
+        node_mlp(layer, (2, 3))
         if layer < LAYERS - 1:
             load_edge_weights(layer + 1)
             load_node_weights(layer + 1)
-        node_norm(layer, hout_ref if layer == LAYERS - 1 else ht)
+        node_norm(layer)
 
         @pl.loop(0, FACES)
         def _(k):
             latents_copy(layer, k).wait_send()
             sums_copy(layer, k).wait_send()
 
-    @pl.loop(0, FACES // 2)
-    def _(q):
-        edges_out(q).wait()
-
-
-def turn_kernel(ht_ref, et_ref, h_ref, e_ref):
-    width = ht_ref.shape[0]
-    for i in range(ht_ref.shape[1] // TILE):
-        h_ref[i * TILE:(i + 1) * TILE, :] = ht_ref[:, i * TILE:(i + 1) * TILE].T
-        for k in range(FACES):
-            first = (i * FACES + k) * TILE
-            e_ref[first:first + TILE, :] = et_ref[i, k].T
+
+def place_kernel(h_in, e_in, h_ref, e_ref, sems):
+    parts = sems.shape[0] - 1
+    rows = e_in.shape[0] // parts
+    copies = [pltpu.make_async_copy(e_in.at[pl.ds(i * rows, rows)], e_ref.at[pl.ds(i * rows, rows)], sems.at[i])
+              for i in range(parts)]
+    copies.append(pltpu.make_async_copy(h_in, h_ref, sems.at[parts]))
+    for copy in copies:
+        copy.start()
+    for copy in copies:
+        copy.wait()
 
 
 def per_device(n, node_latent, edge_latent, edge_ends, edge_owned, send_index, edge_w1, edge_b1, edge_w2,
@@ -382,20 +424,21 @@
     halo_rows = send_index.shape[2]
     groups = own_rows // TILE
     vmem = pl.BlockSpec(memory_space=VMEM)
-    anywhere = pl.BlockSpec(memory_space=pl.ANY)
     faces = (LAYERS, FACES, width, halo_rows)
     sems = pltpu.SemaphoreType.DMA((LAYERS, FACES))
     peers = pltpu.SemaphoreType.DMA((LAYERS, n))
-    ht, et = pl.pallas_call(
+    inputs = (node_latent, edge_latent, edge_ends, edge_owned.reshape(1, slots), send_index.reshape(1, FACES * halo_rows),
+              edge_w1, edge_b1, edge_w2, edge_gain, edge_shift, node_w1, node_b1, node_w2, node_gain, node_shift)
+    inputs = [pltpu.with_memory_space_constraint(a, pltpu.HBM) for a in inputs]
+    nodes, edges = pl.pallas_call(
         functools.partial(mesh_kernel, n),
-        in_specs=[vmem, anywhere] + [vmem] * 13,
-        out_specs=[vmem, anywhere],
-        out_shape=[jax.ShapeDtypeStruct((width, own_rows), BF16),
+        in_specs=[pl.BlockSpec(memory_space=pltpu.HBM)] * len(inputs),
+        out_specs=[vmem, vmem],
+        out_shape=[jax.ShapeDtypeStruct((own_rows, width), BF16),
                    jax.ShapeDtypeStruct((groups, FACES, width, TILE), BF16)],
-        scratch_shapes=[
-            VMEM((width, own_rows), BF16),
+        scratch_shapes=[VMEM(a.shape, a.dtype) for i, a in enumerate(inputs) if i != 1] + [
+            VMEM((2 * width, own_rows), BF16), VMEM((FACES, 2 * width, halo_rows), F32),
             VMEM((slots, width), BF16),
-            VMEM((groups, FACES, width, TILE), BF16),
             VMEM((UNITS, 2, width, 2 * TILE), BF16),
             VMEM((groups, width, 2 * TILE), BF16),
             VMEM((2, 2 * width, halo_rows), BF16),
@@ -411,24 +454,21 @@
             VMEM((width, width), BF16),
             VMEM(faces, BF16), VMEM(faces, BF16), VMEM(faces, BF16), VMEM(faces, BF16),
             VMEM((2, width, TILE), F32), VMEM((LAYERS, 2, width), F32), VMEM((LAYERS, n, 2, width), F32),
-            pltpu.SemaphoreType.DMA, pltpu.SemaphoreType.DMA((FACES // 2,)),
+            pltpu.SemaphoreType.DMA, pltpu.SemaphoreType.DMA((len(inputs) - 1,)),
             sems, sems, sems, sems, peers, peers,
         ],
-        compiler_params=pltpu.CompilerParams(collective_id=0, has_side_effects=True),
-    )(node_latent, edge_latent, edge_ends, edge_owned.reshape(1, slots), send_index.reshape(1, FACES * halo_rows),
-      edge_w1, edge_b1, edge_w2, edge_gain, edge_shift, node_w1, node_b1, node_w2, node_gain, node_shift)
-    per = 4 if groups % 4 == 0 else 1
+        compiler_params=pltpu.CompilerParams(collective_id=0, has_side_effects=True, vmem_limit_bytes=44 * 2 ** 20),
+    )(*inputs)
+    results = [pltpu.with_memory_space_constraint(a, pltpu.VMEM) for a in (nodes, edges.reshape(slots, width))]
+    parts = 6
     return pl.pallas_call(
-        turn_kernel,
-        grid=(groups // per,),
-        in_specs=[pl.BlockSpec((width, per * TILE), lambda i: (0, i)),
-                  pl.BlockSpec((per, FACES, width, TILE), lambda i: (i, 0, 0, 0))],
-        out_specs=[pl.BlockSpec((per * TILE, width), lambda i: (i, 0)),
-                   pl.BlockSpec((per * FACES * TILE, width), lambda i: (i, 0))],
-        out_shape=[jax.ShapeDtypeStruct((own_rows, width), BF16),
-                   jax.ShapeDtypeStruct((slots, width), BF16)],
-        compiler_params=pltpu.CompilerParams(dimension_semantics=("arbitrary",)),
-    )(ht, et)
+        place_kernel,
+        in_specs=[vmem, vmem],
+        out_specs=[pl.BlockSpec(memory_space=pltpu.HBM)] * 2,
+        out_shape=[jax.ShapeDtypeStruct((own_rows, width), BF16), jax.ShapeDtypeStruct((slots, width), BF16)],
+        scratch_shapes=[pltpu.SemaphoreType.DMA((parts + 1,))],
+        compiler_params=pltpu.CompilerParams(vmem_limit_bytes=4 * 2 ** 20),
+    )(*results)
 
 
 def solution(mesh):

time: 95 us -> 75.3 us (0.79)
  Pallas kernels: 94 us -> 74.4 us
    pallas_call x2, Pallas kernels: 94 us -> 74.4 us  [the longest x1 71.3 us: per_device(): pl.pallas_call(functools.partial(mesh_kernel, n), in_specs=[pl.BlockSpec(...]
where the time goes in v2:
time: 75.3 us; the launch traced here: 75.2 us
  Pallas kernels  74.4 us (99%)
  between operations  0.8 us (1%)
    pallas_call x1, Pallas kernels, per_device(): pl.pallas_call(functools.partial(mesh_kernel, n), in_specs=[pl.BlockSpec(...  71.3 us
    pallas_call x1, Pallas kernels, per_device(): pl.pallas_call(place_kernel, in_specs=[vmem, vmem], out_specs=[pl.BlockSp...  3.04 us

profile of v2, /device:TPU:0, one launch (start us, length us, event | category | flops | bytes accessed | tf_op | source)
XLA Modules:
  0.0 75.2 jit_solution(3625614506070294074)
XLA Ops:
  0.6 71.3 %shard_map.158 = (bf16[4096,128]{1,0:T(8,128)(2,1)S(1)}, bf16[32,6,128,128]{3,2,1,0:T(8,128)(2,1)S(1)}) custom-call(bf16[4096,128]{1,0:T(8,128)(2,1)} %h_in.1, bf16[24576,128]{1,0:T(8,128)(2,1)} %e_ref.1, s32[2,24576]{1,0:T(2,128)} %ends_in.1, s32[1,24576]{1,0:T(1,128)} %bitcast.4, s32[1,1536]{1,0:T(1,128)} %bitcast.5, bf16[2,384,128]{2,1,0:T(8,128)(2,1)} %ew1_in.1, ...), custom_call_target="tpu_custom_call" | custom-call | tf_op jit(solution)/shard_map/pallas_call | solution.py:433
  72.0 3.0 %shard_map.159 = (bf16[4096,128]{1,0:T(8,128)(2,1)}, bf16[24576,128]{1,0:T(8,128)(2,1)}) custom-call(bf16[4096,128]{1,0:T(8,128)(2,1)S(1)} %get-tuple-element.4.h_in, bf16[24576,128]{1,0:T(8,128)(2,1)S(1)} %bitcast.3), custom_call_target="tpu_custom_call" | custom-call | tf_op jit(solution)/shard_map/pallas_call | solution.py:464

commit v3 on v2

--- a/solution.py
+++ b/solution.py
@@ -13,8 +13,8 @@
 GY = 4
 TILE = 128
 UNITS = 16
-LAG = 2
-SPAN = 2
+LAG = 1
+SPAN = 1
 CHUNKS = 8
 MESH = pl.DeviceIdType.MESH
 VMEM = pltpu.VMEM
@@ -66,7 +66,7 @@
                 hout_ref, et,
                 h_ref, ends_ref, owned_ref, send_ref, ew1_ref, eb1_ref, ew2_ref, egain_ref, eshift_ref,
                 nw1_ref, nb1_ref, nw2_ref, ngain_ref, nshift_ref,
-                ht, ahead, estage, hid, ptab, phalo, own_acc, halo_acc, upd, scol, w1e, w1sr, w2c, cols, nw1, nw2,
+                ht, soon, ahead, estage, hid, ptab, phalo, own_acc, halo_acc, upd, scol, w1e, w1sr, w2c, cols, nw1, nw2,
                 stage, landed, hsend, returned, sums, mine, stats,
                 esem, isem, lsend, lrecv, bsend, brecv, tsem, usem):
     inputs = [(h_in, h_ref), (send_in, send_ref), (ew1_in, ew1_ref), (eb1_in, eb1_ref), (ew2_in, ew2_ref),
@@ -104,26 +104,26 @@
 
     loads[0].wait()
     for i in range(groups):
-        ht[0:width, i * TILE:(i + 1) * TILE] = h_ref[i * TILE:(i + 1) * TILE, :].T
+        ht[:, i * TILE:(i + 1) * TILE] = h_ref[i * TILE:(i + 1) * TILE, :].T
     for load in loads[1:]:
         load.wait()
     for j in range(FACES * halo_rows // TILE):
         row = send_ref[0:1, j * TILE:(j + 1) * TILE]
-        scol[j * TILE:(j + 1) * TILE, :] = column(row).astype(I16)
-
-    def gather(k0, rows):
+        scol[j * TILE:(j + 1) * TILE, :] = column(row)
+
+    def gather(k0, source):
         totals = [None] * 2
         picks = [send_ref[0:1, pl.ds(pl.multiple_of((k0 + f) * halo_rows, TILE), halo_rows)] for f in range(2)]
         for b in range(own_rows // 256):
             for f in range(2):
-                part = dot(ht[0:rows, b * 256:(b + 1) * 256], hot_rows(picks[f] - b * 256, 256))
+                part = dot(source[:, b * 256:(b + 1) * 256], hot_rows(picks[f] - b * 256, 256))
                 totals[f] = part if totals[f] is None else totals[f] + part
         return totals
 
     def send_first():
         for phase in range(FACES // 2):
             k0 = 2 * (2 * phase % (FACES // 2))
-            totals = gather(k0, width)
+            totals = gather(k0, ht)
             if phase == 0:
                 pl.semaphore_wait(barrier, n - 1)
             for f in range(2):
@@ -133,7 +133,7 @@
     def gather_ahead():
         @pl.loop(0, FACES // 2)
         def _(q):
-            totals = gather(2 * q, 2 * width)
+            totals = gather(2 * q, soon)
             for f in range(2):
                 ahead[2 * q + f] = totals[f]
 
@@ -142,7 +142,8 @@
         def _(p):
             k0 = 2 * face_pair(p)
             for f in range(2):
-                new = ahead[k0 + f, 0:width] + twice(cols[4]) * ahead[k0 + f, width:2 * width] + twice(cols[5])
+                old = stage[layer - 1, k0 + f].astype(F32)
+                new = old + twice(cols[4]) * ahead[k0 + f] + twice(cols[5])
                 stage[layer, pl.ds(k0 + f, 1)] = new.astype(BF16)[None]
                 latents_copy(layer, k0 + f).start()
 
@@ -177,7 +178,7 @@
         def _(c):
             for half in range(2):
                 first = pl.multiple_of((c * 2 + half) * chunk, chunk)
-                both = dot(w1sr[...], ht[0:width, pl.ds(first, chunk)])
+                both = dot(w1sr[...], ht[:, pl.ds(first, chunk)])
                 both = (both + twice(twice(jnp.concatenate([cols[0], cols[0]], axis=0)))).astype(BF16)
                 for j in range(4):
                     at = slice(j * TILE, (j + 1) * TILE)
@@ -219,13 +220,7 @@
         return jnp.concatenate([pick(pair * 2, face), pick(pair * 2 + 1, face)], axis=1)
 
     def gather_stage(layer, u, pair, k0):
-        from_halo = [[None] * 2, [None] * 2]
-        for f in range(2):
-            both = dot(phalo[f], hot_rows(both_groups(halo_row, pair, k0 + f), halo_rows))
-            for g in range(2):
-                part = both[:, g * TILE:(g + 1) * TILE]
-                flag = jnp.broadcast_to(halo_flag(pair * 2 + g, k0 + f), (width, TILE)) > 0.5
-                from_halo[g][f] = jnp.where(flag, part[width:], part[:width])
+        own = []
         for g in range(2):
             group = pair * 2 + g
             old = []
@@ -240,7 +235,16 @@
                                     hot_rows(both_tiles(receive_row, group, k0), TILE),
                                     jnp.concatenate(old, axis=1)], axis=0)
             before = dot(jnp.concatenate([ptab[group], w1e[...]], axis=1), hots)
-            before = before + jnp.concatenate(from_halo[g], axis=1)
+            own.append(before)
+        from_halo = [[None] * 2, [None] * 2]
+        for f in range(2):
+            both = dot(phalo[f], hot_rows(both_groups(halo_row, pair, k0 + f), halo_rows))
+            for g in range(2):
+                part = both[:, g * TILE:(g + 1) * TILE]
+                flag = jnp.broadcast_to(halo_flag(pair * 2 + g, k0 + f), (width, TILE)) > 0.5
+                from_halo[g][f] = jnp.where(flag, part[width:], part[:width])
+        for g in range(2):
+            before = own[g] + jnp.concatenate(from_halo[g], axis=1)
             hid[u, g] = jnp.maximum(before, 0.0).astype(BF16)
 
     def mix_stage(layer, u, pair, k0):
@@ -297,7 +301,7 @@
         for j in range(2):
             goal = (lane + (base + j * TILE)).astype(I16)
             hots.append(jnp.concatenate(
-                [jnp.where(scol[k * halo_rows:(k + 1) * halo_rows, :] == goal, jnp.ones((), BF16), jnp.zeros((), BF16))
+                [jnp.where(scol[k * halo_rows:(k + 1) * halo_rows, :].astype(I16) == goal, jnp.ones((), BF16), jnp.zeros((), BF16))
                  for k in faces], axis=0))
         values = jnp.concatenate([returned[layer, k] for k in faces], axis=1)
         return dot(values, jnp.concatenate(hots, axis=1))
@@ -327,7 +331,7 @@
                 own = jnp.concatenate([own_acc[pair * 2], own_acc[pair * 2 + 1]], axis=1)
                 agg = (own + slots(layer, faces, pair * 256)).astype(BF16)
                 at = pl.ds(pl.multiple_of(pair * 256, 256), 256)
-                joined.append(jnp.concatenate([ht[0:width, at], agg], axis=0))
+                joined.append(jnp.concatenate([ht[:, at], agg], axis=0))
             for i in range(CHUNKS):
                 hidden.append(jnp.maximum(dot(nw1[...], joined[i]) + twice(cols[3]), 0.0).astype(BF16))
             for i in range(CHUNKS):
@@ -335,7 +339,7 @@
                 at = pl.ds(pl.multiple_of((c * CHUNKS + i) * 256, 256), 256)
                 upd[:, at] = update
                 if layer < LAYERS - 1:
-                    ht[width:2 * width, at] = update.astype(BF16)
+                    soon[:, at] = update.astype(BF16)
                 square = update * update
                 sums[0] += update[:, :TILE] + update[:, TILE:]
                 sums[1] += square[:, :TILE] + square[:, TILE:]
@@ -373,11 +377,11 @@
         def _(c):
             for half in range(2):
                 at = pl.ds(pl.multiple_of((c * 2 + half) * 256, 256), 256)
-                new = (ht[0:width, at].astype(F32) + twice(cols[4]) * upd[:, at] + twice(cols[5])).astype(BF16)
+                new = (ht[:, at].astype(F32) + twice(cols[4]) * upd[:, at] + twice(cols[5])).astype(BF16)
                 if last:
                     hout_ref[at, :] = new.T
                 else:
-                    ht[0:width, at] = new
+                    ht[:, at] = new
 
     load_edge_weights(0)
     load_node_weights(0)
@@ -437,7 +441,7 @@
         out_shape=[jax.ShapeDtypeStruct((own_rows, width), BF16),
                    jax.ShapeDtypeStruct((groups, FACES, width, TILE), BF16)],
         scratch_shapes=[VMEM(a.shape, a.dtype) for i, a in enumerate(inputs) if i != 1] + [
-            VMEM((2 * width, own_rows), BF16), VMEM((FACES, 2 * width, halo_rows), F32),
+            VMEM((width, own_rows), BF16), VMEM((width, own_rows), BF16), VMEM((FACES, width, halo_rows), F32),
             VMEM((slots, width), BF16),
             VMEM((UNITS, 2, width, 2 * TILE), BF16),
             VMEM((groups, width, 2 * TILE), BF16),
@@ -445,7 +449,7 @@
             VMEM((groups, width, TILE), F32),
             VMEM((2, width, halo_rows), F32),
             VMEM((width, own_rows), F32),
-            VMEM((FACES * halo_rows, TILE), I16),
+            VMEM((FACES * halo_rows, TILE), I32),
             VMEM((width, width), BF16),
             VMEM((2 * width, width), BF16),
             VMEM((width, width), BF16),

time: 75.3 us -> 74.7 us (level)
  no operation moved by 1% of the time
where the time goes in v3:
time: 74.7 us; the launch traced here: 74.5 us
  Pallas kernels  73.7 us (99%)
  between operations  0.8 us (1%)
    pallas_call x1, Pallas kernels, per_device(): pl.pallas_call(functools.partial(mesh_kernel, n), in_specs=[pl.BlockSpec(...  70.7 us
    pallas_call x1, Pallas kernels, per_device(): pl.pallas_call(place_kernel, in_specs=[vmem, vmem], out_specs=[pl.BlockSp...  3.04 us

profile of v3, /device:TPU:0, one launch (start us, length us, event | category | flops | bytes accessed | tf_op | source)
XLA Modules:
  0.0 74.5 jit_solution(14709834514308867918)
XLA Ops:
  0.6 70.7 %shard_map.158 = (bf16[4096,128]{1,0:T(8,128)(2,1)S(1)}, bf16[32,6,128,128]{3,2,1,0:T(8,128)(2,1)S(1)}) custom-call(bf16[4096,128]{1,0:T(8,128)(2,1)} %h_in.1, bf16[24576,128]{1,0:T(8,128)(2,1)} %e_ref.1, s32[2,24576]{1,0:T(2,128)} %ends_in.1, s32[1,24576]{1,0:T(1,128)} %bitcast.4, s32[1,1536]{1,0:T(1,128)} %bitcast.5, bf16[2,384,128]{2,1,0:T(8,128)(2,1)} %ew1_in.1, ...), custom_call_target="tpu_custom_call" | custom-call | tf_op jit(solution)/shard_map/pallas_call | solution.py:437
  71.3 3.0 %shard_map.159 = (bf16[4096,128]{1,0:T(8,128)(2,1)}, bf16[24576,128]{1,0:T(8,128)(2,1)}) custom-call(bf16[4096,128]{1,0:T(8,128)(2,1)S(1)} %get-tuple-element.4.h_in, bf16[24576,128]{1,0:T(8,128)(2,1)S(1)} %bitcast.3), custom_call_target="tpu_custom_call" | custom-call | tf_op jit(solution)/shard_map/pallas_call | solution.py:468

commit v4 on v3

--- a/solution.py
+++ b/solution.py
@@ -171,20 +171,26 @@
         nw2[...] = nw2_ref[layer].T
         cols[3] = column(nb1_ref[layer:layer + 1, :])
 
-    def own_tables():
+    def own_tables(fresh):
         chunk = 4 * TILE
-
-        @pl.loop(0, own_rows // chunk // 2)
+        parts = 4 if own_rows // chunk % 4 == 0 else 1
+
+        @pl.loop(0, own_rows // chunk // parts)
         def _(c):
-            for half in range(2):
-                first = pl.multiple_of((c * 2 + half) * chunk, chunk)
-                both = dot(w1sr[...], ht[:, pl.ds(first, chunk)])
+            for part in range(parts):
+                index = c * parts + part
+                at = pl.ds(pl.multiple_of(index * chunk, chunk), chunk)
+                nodes = ht[:, at]
+                if fresh:
+                    scale, offset = [twice(twice(cols[i])) for i in (4, 5)]
+                    nodes = (nodes.astype(F32) + scale * upd[:, at] + offset).astype(BF16)
+                    ht[:, at] = nodes
+                both = dot(w1sr[...], nodes)
                 both = (both + twice(twice(jnp.concatenate([cols[0], cols[0]], axis=0)))).astype(BF16)
                 for j in range(4):
-                    at = slice(j * TILE, (j + 1) * TILE)
-                    ptab[pl.ds((c * 2 + half) * 4 + j, 1)] = jnp.concatenate(
-                        [both[:width, at], both[width:, at]], axis=1)[None]
-                    own_acc[pl.ds((c * 2 + half) * 4 + j, 1)] = jnp.zeros((1, TILE, TILE), F32)
+                    lanes = slice(j * TILE, (j + 1) * TILE)
+                    ptab[pl.ds(index * 4 + j, 1)] = jnp.concatenate([both[:width, lanes], both[width:, lanes]], axis=1)[None]
+                    own_acc[pl.ds(index * 4 + j, 1)] = jnp.zeros((1, TILE, TILE), F32)
 
     def ends_of(group, face):
         first = pl.multiple_of((group * FACES + face) * TILE, TILE)
@@ -372,22 +378,20 @@
         cols[5] = column(nshift_ref[layer:layer + 1, :] - scale * mean)
         if not last:
             send_next(layer + 1)
+            return
 
         @pl.loop(0, own_rows // 512)
         def _(c):
             for half in range(2):
                 at = pl.ds(pl.multiple_of((c * 2 + half) * 256, 256), 256)
-                new = (ht[:, at].astype(F32) + twice(cols[4]) * upd[:, at] + twice(cols[5])).astype(BF16)
-                if last:
-                    hout_ref[at, :] = new.T
-                else:
-                    ht[:, at] = new
+                new = ht[:, at].astype(F32) + twice(cols[4]) * upd[:, at] + twice(cols[5])
+                hout_ref[at, :] = new.astype(BF16).T
 
     load_edge_weights(0)
     load_node_weights(0)
     send_first()
     for layer in range(LAYERS):
-        own_tables()
+        own_tables(layer > 0)
         if layer == 0:
             edges_in.wait()
 

time: 74.7 us -> 74.7 us (level)
  no operation moved by 1% of the time
where the time goes in v4:
time: 74.7 us; the launch traced here: 74.5 us
  Pallas kernels  73.7 us (99%)
  between operations  0.8 us (1%)
    pallas_call x1, Pallas kernels, per_device(): pl.pallas_call(functools.partial(mesh_kernel, n), in_specs=[pl.BlockSpec(...  70.7 us
    pallas_call x1, Pallas kernels, per_device(): pl.pallas_call(place_kernel, in_specs=[vmem, vmem], out_specs=[pl.BlockSp...  3.04 us

profile of v4, /device:TPU:0, one launch (start us, length us, event | category | flops | bytes accessed | tf_op | source)
XLA Modules:
  0.0 74.5 jit_solution(2399187629734751669)
XLA Ops:
  0.6 70.7 %shard_map.158 = (bf16[4096,128]{1,0:T(8,128)(2,1)S(1)}, bf16[32,6,128,128]{3,2,1,0:T(8,128)(2,1)S(1)}) custom-call(bf16[4096,128]{1,0:T(8,128)(2,1)} %h_in.1, bf16[24576,128]{1,0:T(8,128)(2,1)} %e_ref.1, s32[2,24576]{1,0:T(2,128)} %ends_in.1, s32[1,24576]{1,0:T(1,128)} %bitcast.4, s32[1,1536]{1,0:T(1,128)} %bitcast.5, bf16[2,384,128]{2,1,0:T(8,128)(2,1)} %ew1_in.1, ...), custom_call_target="tpu_custom_call" | custom-call | tf_op jit(solution)/shard_map/pallas_call | solution.py:441
  71.3 3.0 %shard_map.159 = (bf16[4096,128]{1,0:T(8,128)(2,1)}, bf16[24576,128]{1,0:T(8,128)(2,1)}) custom-call(bf16[4096,128]{1,0:T(8,128)(2,1)S(1)} %get-tuple-element.4.h_in, bf16[24576,128]{1,0:T(8,128)(2,1)S(1)} %bitcast.3), custom_call_target="tpu_custom_call" | custom-call | tf_op jit(solution)/shard_map/pallas_call | solution.py:472
